TPU v7x, 32 devices: a whole 2x2x4 slice. The times are simulated.
32 devices in a mesh: dp: 4 (over z), seq: 8 (over y, x, core).
Axes of the slice: x: 2, y: 2, z: 4, core: 2. Of those that a mesh axis runs over, the one named last changes fastest.
Arguments:
- projections: bfloat16 [1, 4, 1024, 4096], P(None, 'dp', 'seq'), may hold values from -6 to 6
- rotated_query_gradient: bfloat16 [1, 4, 1024, 4096], P(None, 'dp', None, 'seq'), may hold values from -6 to 6
- gains: float32 [1, 4096], replicated, may hold values from 0.25 to 1.75
- adapter_lowering: bfloat16 [1, 48, 5120], P(None, 'dp'), may hold values from -0.078125 to 0.078125
- adapter_raising: bfloat16 [1, 48, 4096], P(None, 'dp'), may hold values from -0.875 to 0.875
- activations: bfloat16 [4, 1024, 5120], P('dp', 'seq'), may hold values from -6 to 6
- positions: int32 [3, 4, 1024], P(None, 'dp', 'seq'), may hold values from 0 to 22, as said below
- valid: int32 [4, 1024], P('dp', 'seq'), may hold values from 0 to 1, as said below
Outputs:
- grad_down: float32 [1, 48, 5120], P(None, 'dp')
- grad_up: float32 [1, 48, 4096], P(None, 'dp')
- grad_gain: float32 [1, 4096], replicated
Inputs may be any that keep to these rules, and one draw needn't show every extreme that they name: `positions`: within a video the frame index never falls; one frame holds 128 tokens. Every eighth token of a video is valid.
All inputs are finite; a program needn't handle non-finite values.
Results may differ from a plain program's by a relative error of at most 0.0041.
Values may be sent and summed in bfloat16 or wider, within the bound.
A program may use at most 64 MiB of HBM per device.

v0:
```python
import jax
import jax.numpy as jnp
from jax import lax
from jax.sharding import PartitionSpec as P

HD = 128


EPSILON = 1e-06


def rope_tables(positions, head_size):
    one_sixth = head_size // 6
    counts = (head_size // 2 - 2 * one_sixth, one_sixth, one_sixth)
    pieces = []
    for component in range(3):
        frequency = 10000.0 ** (
            -jnp.arange(counts[component], dtype=jnp.float32) / counts[component]
        )
        pieces.append(positions[component].astype(jnp.float32)[..., None] * frequency)
    angles = jnp.concatenate(pieces, -1)
    return (jnp.cos(angles), jnp.sin(angles))


def norm_backward(projections, rotated_query_gradient, gains, positions, valid):
    cosine, sine_table = rope_tables(positions, HD)
    full_shape = rotated_query_gradient.shape
    cotangent = (
        rotated_query_gradient.astype(jnp.float32) * valid.astype(jnp.float32)[None, :, :, None]
    )
    cotangent = cotangent.reshape(full_shape[:3] + (full_shape[3] // HD, HD // 2, 2))
    cosine = cosine[None, :, :, None, :]
    sine_table = sine_table[None, :, :, None, :]
    even_part = cosine * cotangent[..., 0] + sine_table * cotangent[..., 1]
    odd_part = cosine * cotangent[..., 1] - sine_table * cotangent[..., 0]
    unrotated = jnp.stack([even_part, odd_part], -1).reshape(full_shape)
    values = projections.astype(jnp.float32)
    inverse = lax.rsqrt(jnp.mean(values * values, -1, keepdims=True) + EPSILON)
    normed = values * inverse
    gain_part = jnp.sum(unrotated * normed, axis=(1, 2))
    scaled = unrotated * gains[:, None, None, :]
    projection_change = inverse * (scaled - normed * jnp.mean(scaled * normed, -1, keepdims=True))
    return (projection_change.astype(jnp.bfloat16), gain_part)


def adapter_partial_terms(projection_change, input_list, lowering_matrices, raising_matrices):
    reduced = jnp.dot(
        input_list, lowering_matrices[0].T, preferred_element_type=jnp.float32
    ).astype(jnp.bfloat16)
    up_terms = [jnp.dot(reduced.T, projection_change[0], preferred_element_type=jnp.float32)]
    back_rank = jnp.dot(
        projection_change[0], raising_matrices[0].T, preferred_element_type=jnp.float32
    ).astype(jnp.bfloat16)
    down_terms = [jnp.dot(back_rank.T, input_list, preferred_element_type=jnp.float32)]
    return (jnp.stack(down_terms), jnp.stack(up_terms))


def shards(
    projections,
    rotated_query_gradient,
    gains,
    adapter_lowering,
    adapter_raising,
    activations,
    positions,
    valid,
):
    local_count = jnp.sum(valid.astype(jnp.float32))
    total_count = lax.psum(local_count, ("dp", "seq"))
    token_grad = lax.all_to_all(
        rotated_query_gradient, "seq", split_axis=2, concat_axis=3, tiled=True
    )
    lowering_complete, raising_complete = (
        lax.all_gather(adapter_lowering, "dp", axis=1, tiled=True),
        lax.all_gather(adapter_raising, "dp", axis=1, tiled=True),
    )
    projection_change, gain_part = norm_backward(projections, token_grad, gains, positions, valid)
    lowering_portion, raising_portion = adapter_partial_terms(
        projection_change[:, 0], activations[0], lowering_complete, raising_complete
    )
    down_share, up_share = (
        lax.psum_scatter(lowering_portion, "seq", scatter_dimension=2, tiled=True),
        lax.psum_scatter(raising_portion, "seq", scatter_dimension=2, tiled=True),
    )
    down_share, up_share = (
        lax.psum_scatter(down_share, "dp", scatter_dimension=1, tiled=True),
        lax.psum_scatter(up_share, "dp", scatter_dimension=1, tiled=True),
    )
    down_sum, up_sum = (
        lax.all_gather(down_share, "seq", axis=2, tiled=True),
        lax.all_gather(up_share, "seq", axis=2, tiled=True),
    )
    gain_total = lax.psum(gain_part, ("dp", "seq"))
    all_tokens = lax.axis_size("dp") * lax.axis_size("seq") * valid.shape[1]
    factor = jnp.float32(all_tokens) / total_count
    return (factor * down_sum, factor * up_sum, factor * gain_total)


def solution(mesh):
    in_specs = (
        P(None, "dp", "seq", None),
        P(None, "dp", None, "seq"),
        P(),
        P(None, "dp", None),
        P(None, "dp", None),
        P("dp", "seq", None),
        P(None, "dp", "seq"),
        P("dp", "seq"),
    )
    out_specs = (P(None, "dp", None), P(None, "dp", None), P())
    return jax.shard_map(shards, mesh=mesh, in_specs=in_specs, out_specs=out_specs, check_vma=False)
```

profile of v0, /device:TPU:0, one launch (start us, length us, event | category | flops | bytes accessed | tf_op | source)
XLA Modules:
  0.0 216.2 jit_solution(14049534258103671952)
XLA Ops:
  7.2 2.9 %copy.49 = bf16[1,1,1024,512]{3,1,0,2:T(2,128)(2,1)S(1)} copy(bf16[1,1,1024,512]{3,2,1,0:T(8,128)(2,1)} %param.9) | data formatting | bytes 2097152 | tf_op args[1]
  10.6 8.1 %reduce.3 = bf16[1024,512]{1,0:T(8,128)(2,1)} reduce(bf16[1024,1,1,512]{3,2,1,0:T(2,128)(2,1)S(1)} %bitcast.49, bf16[]{:T(256)} %broadcast.193), dimensions={1,2}, to_apply=%bitcast.45.reduce_sub_computation | reduce | bytes 2097154
  18.7 2.7 %reshape.359 = bf16[8,2,32768]{2,1,0:T(2,128)(2,1)} reshape(bf16[1024,512]{1,0:T(8,128)(2,1)} %reduce.3) | data formatting | bytes 2097152
  21.4 5.2 %all-to-all-start = ((bf16[8,2,32768]{2,1,0:T(2,128)(2,1)}), bf16[8,2,32768]{2,1,0:T(2,128)(2,1)S(1)}, u32[]{:S(2)}, u32[]{:S(2)}) async-start(bf16[8,2,32768]{2,1,0:T(2,128)(2,1)} %reshape.359), calls=%async_computation | async-start | bytes 2097152 | tf_op jit(solution)/shard_map/all_to_all | solution.py:70
  26.7 1.6 copy.28
  30.3 22.6 %all_gather.14 = bf16[1,48,5120]{2,0,1:T(2,128)(2,1)} all-gather(bf16[1,12,5120]{2,0,1:T(2,128)(2,1)S(1)} %copy.34), channel_id=1, replica_groups=mesh['dp'=4,'seq'=8] {'dp'}, dimensions={1}, use_global_device_ids=true | all-gather | bytes 614400 | tf_op jit(solution)/shard_map/all_gather | solution.py:74
  52.9 3.5 %reshape.360 = bf16[1024,1,1,512]{3,2,1,0:T(2,128)(2,1)} reshape(bf16[8,2,32768]{2,1,0:T(2,128)(2,1)S(1)} %all-to-all-done) | data formatting | bytes 2097152
  56.4 1.9 copy.30
  58.2 1.6 convert_bitcast_fusion
  59.9 2.9 %copy.31 = f32[1,1,128,8,512]{2,4,3,1,0:T(8,128)} copy(f32[1,1,128,8,512]{4,2,3,1,0:T(8,128)} %convert_bitcast_fusion) | data formatting | bytes 4194304 | tf_op jit(solution)/shard_map/convert_element_type | solution.py:29
  62.8 2.4 %broadcast_multiply_fusion = f32[1,1,128,32,64,2]{2,5,4,3,1,0:T(2,128)S(1)} fusion(f32[1,1,128,32,64,2]{2,5,4,3,1,0:T(2,128)} %bitcast.50, f32[128]{0:T(128)S(1)} %convert_bitcast_fusion.4), kind=kLoop, calls=%fused_computation.23 | loop fusion | flops 524288 | bytes 4194816 | tf_op jit(solution)/shard_map/mul | solution.py:29
  65.2 2.6 %multiply_add_fusion = (f32[1,1,128,32,64,1]{2,5,4,3,1,0:T(1,128)S(1)}, f32[1,1,128,32,64,1]{2,5,4,3,1,0:T(1,128)S(1)}) fusion(f32[1,1,128,32,64,2]{2,5,4,3,1,0:T(2,128)S(1)} %broadcast_multiply_fusion, f32[128,64]{0,1:T(8,128)S(1)} %get-tuple-element.21, f32[128,64]{0,1:T(8,128)S(1)} %get-tuple-element.20), kind=kLoop, calls=%fused_computation.22 | loop fusion | flops 1572864 | bytes 4259840 | tf_op jit(solution)/shard_map/add | solution.py:34
  67.8 2.0 pad_maximum_fusion
  69.8 1.3 fusion.7
  71.9 3.5 %convolution_bitcast_fusion.1 = f32[1,48,4096]{2,1,0:T(8,128)} fusion(bf16[128,4096]{0,1:T(8,128)(2,1)S(1)} %fusion.15, bf16[1,128,5120]{2,1,0:T(8,128)(2,1)S(1)} %copy-done, bf16[1,48,5120]{2,0,1:T(2,128)(2,1)} %all_gather.14), kind=kOutput, calls=%fused_computation.1 | convolution fusion | flops 113252352 | bytes 3637248 | tf_op jit(solution)/shard_map/dot_general | solution.py:50
  75.7 18.8 %all_gather.12 = bf16[1,48,4096]{2,0,1:T(2,128)(2,1)S(1)} all-gather(bf16[1,12,4096]{2,0,1:T(2,128)(2,1)S(1)} %copy.32), channel_id=1, replica_groups=mesh['dp'=4,'seq'=8] {'dp'}, dimensions={1}, use_global_device_ids=true | all-gather | bytes 491520 | tf_op jit(solution)/shard_map/all_gather | solution.py:75
  94.5 1.8 convolution_bitcast_fusion
  98.2 39.1 %all-reduce.2 = (f32[]{:T(128)}, f32[1,4096]{1,0:T(1,128)S(1)}) all-reduce(f32[]{:T(128)} %convert_reduce_fusion, f32[1,4096]{1,0:T(1,128)S(1)} %bitcast.54), channel_id=1, replica_groups=mesh['dp'=4,'seq'=8] {'dp','seq'}, use_global_device_ids=true, to_apply=%region_1.0 | all-reduce | flops 4097 | bytes 32776 | tf_op jit(solution)/shard_map/psum | solution.py:69
  138.1 1.6 copy.35
  139.7 9.6 %reduce-scatter.3.cloned.1.call-done = f32[1,48,640]{2,1,0:T(8,128)} async-done(((f32[1,48,5120]{2,1,0:T(8,128)}), f32[1,48,640]{2,1,0:T(8,128)}) %reduce-scatter.3.cloned.1.call-update) | async-done | bytes 122896 | tf_op jit(solution)/shard_map/reduce_scatter | solution.py:82
  149.4 1.7 copy.33
  151.7 35.8 %all-reduce.6.cloned.1.call-done = (f32[1,48,640]{2,0,1:T(1,128)}, f32[1,48,512]{2,0,1:T(1,128)}) async-done(((f32[1,48,640]{2,0,1:T(1,128)}, f32[1,48,512]{2,0,1:T(1,128)}), (f32[1,48,640]{2,0,1:T(1,128)}, f32[1,48,512]{2,0,1:T(1,128)})) %all-reduce.6.cloned.1.call-update) | async-done | bytes 221200
  188.2 9.2 %all_gather.15 = f32[1,12,4096]{2,0,1:T(1,128)S(1)} all-gather(f32[1,12,512]{2,0,1:T(1,128)S(1)} %constant_dynamic-slice_fusion), channel_id=1, replica_groups=mesh['dp'=4,'seq'=8] {'seq'}, dimensions={2}, use_global_device_ids=true | all-gather | bytes 221184 | tf_op jit(solution)/shard_map/all_gather | solution.py:91
  199.0 9.8 %all_gather.13 = f32[1,12,5120]{2,0,1:T(1,128)S(1)} all-gather(f32[1,12,640]{2,0,1:T(1,128)S(1)} %constant_dynamic-slice_fusion.1), channel_id=1, replica_groups=mesh['dp'=4,'seq'=8] {'seq'}, dimensions={2}, use_global_device_ids=true | all-gather | bytes 276480 | tf_op jit(solution)/shard_map/all_gather | solution.py:90
  (41 shorter events, 8.6 us)
Async XLA Ops:
  7.2 64.7 %copy-start = (bf16[1,128,5120]{2,1,0:T(8,128)(2,1)S(1)}, bf16[1,128,5120]{2,1,0:T(8,128)(2,1)}, u32[]{:S(2)}) copy-start(bf16[1,128,5120]{2,1,0:T(8,128)(2,1)} %param.13) | copy-start | bytes 3932164
  18.7 7.9 %copy-start.3 = (s32[3,1,128]{2,1,0:T(1,128)S(1)}, s32[3,1,128]{2,1,0:T(1,128)}, u32[]{:S(2)}) copy-start(s32[3,1,128]{2,1,0:T(1,128)} %param.14) | copy-start | bytes 4612
  21.4 31.5 %all-to-all-start = ((bf16[8,2,32768]{2,1,0:T(2,128)(2,1)}), bf16[8,2,32768]{2,1,0:T(2,128)(2,1)S(1)}, u32[]{:S(2)}, u32[]{:S(2)}) async-start(bf16[8,2,32768]{2,1,0:T(2,128)(2,1)} %reshape.359), calls=%async_computation | async-start | bytes 2097152 | tf_op jit(solution)/shard_map/all_to_all | solution.py:70
  26.6 111.5 %reduce-scatter.5.cloned.1.call-start = ((), (), s32[]{:S(2)}) async-start(), calls=%async_computation.4 | async-start | bytes 884736 | tf_op jit(solution)/shard_map/reduce_scatter | solution.py:83
  26.7 26.2 %copy-start.4 = (s32[1,128]{1,0:T(1,128)S(1)}, s32[1,128]{1,0:T(1,128)}, u32[]{:S(2)}) copy-start(s32[1,128]{1,0:T(1,128)} %param.15) | copy-start | bytes 1540
  67.8 2.0 copy-start.2
  71.9 3.6 %copy-start.1 = (bf16[1,12,4096]{2,1,0:T(8,128)(2,1)S(1)}, bf16[1,12,4096]{2,1,0:T(8,128)(2,1)}, u32[]{:S(2)}) copy-start(bf16[1,12,4096]{2,1,0:T(8,128)(2,1)} %param.12) | copy-start | bytes 294916
  75.4 73.9 %reduce-scatter.3.cloned.1.call-start = ((), (), s32[]{:S(2)}) async-start(), calls=%async_computation.3 | async-start | bytes 1105920 | tf_op jit(solution)/shard_map/reduce_scatter | solution.py:82
  94.5 1.9 copy-start.5
  96.3 91.2 %all-reduce.6.cloned.1.call-start = ((), (), s32[]{:S(2)}) async-start(), calls=%async_computation.5 | async-start | bytes 442368
Sparse Core Ops, SparseCore 0:
  75.6 35.2 reduce-scatter.4
  114.1 35.2 reduce-scatter.2
  152.3 35.1 all-reduce.5
where the time goes:
time: 217 us; the launch traced here: 216 us
  blocking collectives  99.5 us (46%)
  waiting for transfers between devices  45.5 us (21%)
  local copies, waits for them, and re-layouts  22.7 us (10%)
  other arithmetic  22.5 us (10%)
  between operations  15.3 us (7%)
  matrix products  5.35 us (2%)
  starting transfers between devices  5.32 us (2%)
    psum x1, blocking collectives, shards(): total_count = lax.psum(local_count, ('dp', 'seq'))  39.1 us
    unnamed x4, waiting for transfers between devices  35.9 us
    all_gather x1, blocking collectives, shards(): lax.all_gather(adapter_lowering, 'dp', axis=1, tiled=True)  22.6 us
    all_gather x1, blocking collectives, shards(): lax.all_gather(adapter_raising, 'dp', axis=1, tiled=True)  18.8 us
    unnamed x22, local copies, waits for them, and re-layouts  14.6 us
    all_gather x1, blocking collectives, shards(): lax.all_gather(down_share, 'seq', axis=2, tiled=True)  9.78 us
    reduce_scatter x1, waiting for transfers between devices, shards(): lax.psum_scatter(lowering_portion, 'seq', scatter_dimension=2, tiled=True)  9.63 us
    all_gather x1, blocking collectives, shards(): lax.all_gather(up_share, 'seq', axis=2, tiled=True)  9.15 us
  transfers between devices with their start and end apart: 4, of which 2 were waited for; matrix products, arithmetic and copies ran while one was open for 4% of the time, Pallas kernels for 0%

commit v1 on v0

v1 whole, which is shorter than its diff:
```python
import functools

import jax
import jax.numpy as jnp
import numpy as np
from jax import lax
from jax.experimental import pallas as pl
from jax.experimental.pallas import tpu as pltpu
from jax.sharding import PartitionSpec as P

HD = 128
EPSILON = 1e-06
LANES = 128
BF = jnp.bfloat16
F32 = jnp.float32
MESH = pl.DeviceIdType.MESH
NT = (((1,), (1,)), ((), ()))


def group_counts():
    one_sixth = HD // 6
    return (HD // 2 - 2 * one_sixth, one_sixth, one_sixth)


def lane_frequencies():
    pieces = []
    for n in group_counts():
        pieces.append(np.float32(10000.0) ** (-np.arange(n, dtype=np.float32) / np.float32(n)))
    return np.repeat(np.concatenate(pieces).astype(np.float32), 2)[None]


def kernel(
    cfg,
    proj_hbm, cot_hbm, act_hbm, adapt_hbm, gains_ref, freq_ref, pos_ref, valid_ref,
    down_ref, up_ref, gain_ref,
    proj, act, cot, adapt, scaled, back_acc, dot_acc, inv_ref, cos_ref, sin_ref, redt, backt,
    small_send, small_recv, small_dp, small_dp_recv, small_fin, small_ag,
    d2d_send_u, d2d_recv_u, own_u, rs_send_u, rs_recv_u, tot_u, dp_send_u, dp_f_u, dp_recv_u, ag_u, fin_u,
    d2d_send_d, d2d_recv_d, own_d, rs_send_d, rs_recv_d, tot_d, dp_send_d, dp_f_d, dp_recv_d, ag_d, fin_d,
    local_sem, cot_s, cot_r, ad_s, ad_r, rel_s, rel_r,
    sm_s, sm_r, smd_s, smd_r, sma_s, sma_r,
    d2d_s, d2d_r, rs_s, rs_r, dp_s, dp_r, ag_s, ag_r,
):
    S, D, T, F, W, R, RP, LH, M, QF = (
        cfg[k] for k in ("S", "D", "T", "F", "W", "R", "RP", "LH", "M", "QF")
    )
    K = S // 2
    ranks = D * R
    hw = 256 if F % 256 == 0 else 128
    d = lax.axis_index("dp")
    s = lax.axis_index("seq")
    c = lax.rem(s, 2)
    chip = s // 2
    sib = s + 1 - 2 * c

    def copy(src, dst, ss, rs, dp, seq):
        return pltpu.make_async_remote_copy(
            src_ref=src, dst_ref=dst, send_sem=ss, recv_sem=rs,
            device_id=(dp, seq), device_id_type=MESH,
        )

    loads = [
        pltpu.make_async_copy(proj_hbm, proj, local_sem.at[0]),
        pltpu.make_async_copy(act_hbm, act.at[:, pl.ds(0, M)], local_sem.at[1]),
        pltpu.make_async_copy(cot_hbm.at[s], cot.at[s], local_sem.at[2]),
        pltpu.make_async_copy(adapt_hbm, adapt.at[d], local_sem.at[3]),
    ]
    for x in loads:
        x.start()

    barrier = pltpu.get_barrier_semaphore()
    for k in range(1, S):
        pl.semaphore_signal(barrier, inc=1, device_id=(d, lax.rem(s + k, S)), device_id_type=MESH)
    for k in range(1, D):
        pl.semaphore_signal(barrier, inc=1, device_id=(lax.rem(d + k, D), s), device_id_type=MESH)
    pl.semaphore_wait(barrier, S + D - 2)

    def cot_copy(peer, slot):
        return copy(cot_hbm.at[peer], cot.at[slot], cot_s.at[peer], cot_r.at[slot], d, peer)

    def adapt_copy(peer, slot):
        return copy(adapt_hbm.at[c], adapt.at[slot, c], ad_s.at[peer], ad_r.at[slot], peer, s)

    def relay_copy(slot, half):
        return copy(adapt.at[slot, half], adapt.at[slot, half], rel_s.at[slot], rel_r.at[slot], d, sib)

    for k in range(1, D):
        adapt_copy(lax.rem(d + k, D), d).start()
    for k in range(1, S):
        cot_copy(lax.rem(s + k, S), s).start()

    n0, n1, _ = group_counts()
    lane = lax.broadcasted_iota(jnp.int32, (T, LANES), 1)

    def column(row):
        return jnp.broadcast_to(row.astype(F32), (LANES, T)).T

    index = jnp.where(
        lane < 2 * n0, column(pos_ref[0:1, :]),
        jnp.where(lane < 2 * (n0 + n1), column(pos_ref[1:2, :]), column(pos_ref[2:3, :])),
    )
    angle = index * freq_ref[...]
    ok = column(valid_ref[...])
    co = jnp.cos(angle) * ok
    si = jnp.sin(angle) * ok
    for i in range(hw // LANES):
        cos_ref[:, i * LANES:(i + 1) * LANES] = co
        sin_ref[:, i * LANES:(i + 1) * LANES] = si
    row_i = lax.broadcasted_iota(jnp.int32, (hw, hw), 0)
    col_i = lax.broadcasted_iota(jnp.int32, (hw, hw), 1)
    even = lax.rem(col_i, 2) == 0
    swap = jnp.where(
        even & (row_i == col_i + 1), 1.0, jnp.where(jnp.logical_not(even) & (row_i == col_i - 1), -1.0, 0.0)
    ).astype(BF)
    count = jnp.sum(valid_ref[...].astype(F32), axis=1, keepdims=True)
    small_send[...] = jnp.broadcast_to(count[:, :, None], small_send.shape)

    loads[0].wait()
    square = jnp.zeros((T, LANES), F32)
    for i in range(QF // LANES):
        v = proj[:, i * LANES:(i + 1) * LANES].astype(F32)
        square += v * v
    inverse = lax.rsqrt(jnp.sum(square, axis=1, keepdims=True) / QF + EPSILON)
    inv_ref[...] = jnp.broadcast_to(inverse, (T, LANES))
    dot_acc[...] = jnp.zeros_like(dot_acc)

    def wide(x):
        return jnp.concatenate([x] * (hw // LANES), axis=1) if hw > LANES else x

    def chunk(p):
        inv = wide(inv_ref[...])
        cw, sw = cos_ref[...], sin_ref[...]
        for i in range(F // hw):
            cols = pl.ds(pl.multiple_of(p * F + i * hw, LANES), hw)
            x = cot[p, :, i * hw:(i + 1) * hw]
            xs = jnp.dot(x, swap, preferred_element_type=F32)
            un = cw * x.astype(F32) + sw * xs
            prod = un * (proj[:, cols].astype(F32) * inv)
            g = jnp.sum(prod, axis=0, keepdims=True)
            for t in range(hw // LANES):
                j = i * (hw // LANES) + t
                small_send[p, j:j + 1, :] = g[:, t * LANES:(t + 1) * LANES]
            gn = gains_ref[:, cols]
            scaled[p, :, i * hw:(i + 1) * hw] = un * gn
            pg = prod * gn
            acc = pg[:, :LANES]
            for t in range(1, hw // LANES):
                acc += pg[:, t * LANES:(t + 1) * LANES]
            dot_acc[...] += acc

    loads[2].wait()
    chunk(s)
    cot_copy(sib, sib).wait_recv()
    chunk(sib)
    loads[3].wait()

    def rest(j, carry):
        p = lax.rem(2 * chip + 2 + j, S)
        cot_copy(p, p).wait_recv()
        chunk(p)
        return carry

    half_rest = (S - 2) // 2
    lax.fori_loop(0, half_rest, rest, 0)
    for k in range(1, D):
        e = lax.rem(d + k, D)
        adapt_copy(e, e).wait_recv()
        relay_copy(e, c).start()
    lax.fori_loop(half_rest, S - 2, rest, 0)

    def small_copy(peer, slot):
        return copy(small_send.at[peer], small_recv.at[slot], sm_s.at[peer], sm_r.at[slot], d, peer)

    for k in range(1, S):
        small_copy(lax.rem(s + k, S), s).start()

    r_i = lax.broadcasted_iota(jnp.int32, (ranks, D * RP), 0)
    q_i = lax.broadcasted_iota(jnp.int32, (ranks, D * RP), 1)
    pick = jnp.where(q_i == (r_i // R) * RP + lax.rem(r_i, R), 1.0, 0.0).astype(BF)

    def dense_transposed(x):
        return lax.dot_general(pick, x.astype(BF), NT, preferred_element_type=F32).astype(BF)

    for k in range(1, D):
        e = lax.rem(d + k, D)
        relay_copy(e, 1 - c).wait_recv()
    loads[1].wait()
    red = jnp.zeros((T, D * RP), F32)
    for h in range(2):
        low = adapt[:, h, :, 0:LH].reshape(D * RP, LH)
        red += lax.dot_general(act[:, h * LH:(h + 1) * LH], low, NT, preferred_element_type=F32)
    redt[...] = dense_transposed(red)

    back_acc[...] = jnp.zeros_like(back_acc)
    dot_mean = jnp.sum(dot_acc[...], axis=1, keepdims=True) / QF
    mean_w = jnp.broadcast_to(dot_mean, (T, LANES))
    dot_acc[...] = mean_w

    def up_term(p):
        inv = wide(inv_ref[...])
        mean = wide(dot_acc[...])
        parts = []
        for i in range(F // hw):
            cols = pl.ds(pl.multiple_of(p * F + i * hw, LANES), hw)
            nrm = proj[:, cols].astype(F32) * inv
            parts.append((inv * (scaled[p, :, i * hw:(i + 1) * hw] - nrm * mean)).astype(BF))
        delta = jnp.concatenate(parts, axis=1) if len(parts) > 1 else parts[0]
        h = p // K
        off = pl.multiple_of(LH + lax.rem(p, K) * F, LANES)
        rai = adapt[:, h, :, pl.ds(off, F)].reshape(D * RP, F)
        back_acc[...] += lax.dot_general(delta, rai, NT, preferred_element_type=F32)
        return jnp.dot(redt[...], delta, preferred_element_type=F32)

    def down_term(p):
        cols = pl.ds(pl.multiple_of(p * W, LANES), W)
        return jnp.dot(backt[...], act[:, cols], preferred_element_type=F32)

    up = dict(i=0, term=up_term, d2d_send=d2d_send_u, d2d_recv=d2d_recv_u, own=own_u,
              rs_send=rs_send_u, rs_recv=rs_recv_u, tot=tot_u, dp_send=dp_send_u, dp_f=dp_f_u,
              dp_recv=dp_recv_u, ag=ag_u, fin=fin_u, out=up_ref, width=F)
    down = dict(i=1, term=down_term, d2d_send=d2d_send_d, d2d_recv=d2d_recv_d, own=own_d,
                rs_send=rs_send_d, rs_recv=rs_recv_d, tot=tot_d, dp_send=dp_send_d, dp_f=dp_f_d,
                dp_recv=dp_recv_d, ag=ag_d, fin=fin_d, out=down_ref, width=W)

    def d2d_copy(b, k):
        i = b["i"]
        return copy(b["d2d_send"].at[k], b["d2d_recv"].at[k], d2d_s.at[i, k], d2d_r.at[i, k], d, sib)

    def rs_copy(b, peer, slot):
        i = b["i"]
        return copy(b["rs_send"].at[peer], b["rs_recv"].at[slot], rs_s.at[i, peer], rs_r.at[i, slot],
                    d, 2 * peer + c)

    def dp_copy(b, peer, slot):
        i = b["i"]
        return copy(b["dp_send"].at[peer], b["dp_recv"].at[slot], dp_s.at[i, peer], dp_r.at[i, slot],
                    peer, s)

    def ag_copy(b, peer, slot):
        i = b["i"]
        return copy(b["fin"], b["ag"].at[slot], ag_s.at[i, peer], ag_r.at[i, slot], d, peer)

    def scatter(b):
        def for_sibling(j, carry):
            k = lax.rem(chip + 1 + j, K)
            b["d2d_send"][k] = b["term"](2 * k + 1 - c).astype(BF)
            d2d_copy(b, k).start()
            return carry

        def for_this_core(j, carry):
            k = lax.rem(chip + 1 + j, K)
            b["own"][k] = b["term"](2 * k + c)
            return carry

        lax.fori_loop(0, K, for_sibling, 0)
        lax.fori_loop(0, K, for_this_core, 0)
        for j in range(1, K):
            k = lax.rem(chip + j, K)
            d2d_copy(b, k).wait_recv()
            b["rs_send"][k] = (b["own"][k] + b["d2d_recv"][k].astype(F32)).astype(BF)
            rs_copy(b, k, chip).start()

    def dp_stage(b):
        d2d_copy(b, chip).wait_recv()
        total = b["own"][chip] + b["d2d_recv"][chip].astype(F32)
        for j in range(1, K):
            q = lax.rem(chip + j, K)
            rs_copy(b, q, q).wait_recv()
            total += b["rs_recv"][q].astype(F32)
        b["tot"][0:ranks, :] = total
        for e in range(D):
            rows = b["tot"][e * R:e * R + RP, :]
            b["dp_f"][e] = rows
            b["dp_send"][e] = rows.astype(BF)
        for k in range(1, D):
            dp_copy(b, lax.rem(d + k, D), d).start()

    def gather(b, factor):
        total = b["dp_f"][d]
        for k in range(1, D):
            e = lax.rem(d + k, D)
            dp_copy(b, e, e).wait_recv()
            total += b["dp_recv"][e].astype(F32)
        fin = (total * factor).astype(BF)
        b["fin"][...] = fin
        for k in range(1, S):
            ag_copy(b, lax.rem(s + k, S), s).start()
        cols = pl.ds(pl.multiple_of(s * b["width"], LANES), b["width"])
        b["out"][:, cols] = fin.astype(F32)[0:R]

    scatter(up)

    small = small_send[s]
    for k in range(1, S):
        q = lax.rem(s + k, S)
        small_copy(q, q).wait_recv()
        small += small_recv[q]
    small_dp[...] = small

    def small_dp_copy(peer, slot):
        return copy(small_dp, small_dp_recv.at[slot], smd_s.at[peer], smd_r.at[slot], peer, s)

    for k in range(1, D):
        small_dp_copy(lax.rem(d + k, D), d).start()

    backt[...] = dense_transposed(back_acc[...])
    scatter(down)
    dp_stage(up)

    small = small_dp[...]
    for k in range(1, D):
        e = lax.rem(d + k, D)
        small_dp_copy(e, e).wait_recv()
        small += small_dp_recv[e]
    groups = F // LANES
    factor = F32(cfg["tokens"]) / small[groups:groups + 1, 0:1]
    small_fin[...] = small * factor

    def small_ag_copy(peer, slot):
        return copy(small_fin, small_ag.at[slot], sma_s.at[peer], sma_r.at[slot], d, peer)

    for k in range(1, S):
        small_ag_copy(lax.rem(s + k, S), s).start()

    dp_stage(down)
    gather(up, factor)
    gather(down, factor)

    def put_gain(q, value):
        for j in range(groups):
            cols = pl.ds(pl.multiple_of(q * F + j * LANES, LANES), LANES)
            gain_ref[:, cols] = value[j:j + 1, :]

    put_gain(s, small_fin[...])
    for k in range(1, S):
        q = lax.rem(s + k, S)
        small_ag_copy(q, q).wait_recv()
        put_gain(q, small_ag[q])
    for b in (up, down):
        for k in range(1, S):
            q = lax.rem(s + k, S)
            ag_copy(b, q, q).wait_recv()
            cols = pl.ds(pl.multiple_of(q * b["width"], LANES), b["width"])
            b["out"][:, cols] = b["ag"][q].astype(F32)[0:R]

    for k in range(1, D):
        e = lax.rem(d + k, D)
        adapt_copy(e, d).wait_send()
        relay_copy(e, c).wait_send()
        small_dp_copy(e, d).wait_send()
        for b in (up, down):
            dp_copy(b, e, d).wait_send()
    for k in range(1, S):
        q = lax.rem(s + k, S)
        cot_copy(q, s).wait_send()
        small_copy(q, s).wait_send()
        small_ag_copy(q, s).wait_send()
        for b in (up, down):
            ag_copy(b, q, s).wait_send()
    for b in (up, down):
        d2d_copy(b, chip).wait_send()
        for j in range(1, K):
            k = lax.rem(chip + j, K)
            d2d_copy(b, k).wait_send()
            rs_copy(b, k, chip).wait_send()


def shards(projections, rotated_query_gradient, gains, adapter_lowering, adapter_raising,
           activations, positions, valid):
    D, S = lax.axis_size("dp"), lax.axis_size("seq")
    T, QF = projections.shape[2:]
    F = rotated_query_gradient.shape[3]
    R, M = adapter_lowering.shape[1:]
    W = -(-M // (LANES * S)) * LANES
    RP = -(-R // 16) * 16
    LH, UH = M // 2, QF // 2
    K = S // 2
    ranks = D * R
    cfg = dict(S=S, D=D, T=T, F=F, W=W, R=R, RP=RP, LH=LH, M=M, QF=QF, tokens=D * S * T)

    low, rai = adapter_lowering[0], adapter_raising[0]
    adapt = jnp.stack(
        [jnp.concatenate([low[:, h * LH:(h + 1) * LH], rai[:, h * UH:(h + 1) * UH]], 1) for h in range(2)]
    )
    adapt = jnp.pad(adapt, ((0, 0), (0, RP - R), (0, 0)))

    def stage(width):
        return [
            pltpu.VMEM((K, ranks, width), BF),
            pltpu.VMEM((K, ranks, width), BF),
            pltpu.VMEM((K, ranks, width), F32),
            pltpu.VMEM((K, ranks, width), BF),
            pltpu.VMEM((K, ranks, width), BF),
            pltpu.VMEM((ranks + RP, width), F32),
            pltpu.VMEM((D, RP, width), BF),
            pltpu.VMEM((D, RP, width), F32),
            pltpu.VMEM((D, RP, width), BF),
            pltpu.VMEM((S, RP, width), BF),
            pltpu.VMEM((RP, width), BF),
        ]

    hw = 256 if F % 256 == 0 else 128
    dma = pltpu.SemaphoreType.DMA
    any_space = pl.BlockSpec(memory_space=pl.ANY)
    vmem = pl.BlockSpec(memory_space=pltpu.VMEM)
    small_rows = -(-(F // LANES + 1) // 8) * 8
    down, up, gain = pl.pallas_call(
        functools.partial(kernel, cfg),
        out_shape=(
            jax.ShapeDtypeStruct((R, S * W), F32),
            jax.ShapeDtypeStruct((R, QF), F32),
            jax.ShapeDtypeStruct((1, QF), F32),
        ),
        in_specs=[any_space] * 4 + [vmem] * 4,
        out_specs=(vmem, vmem, vmem),
        scratch_shapes=[
            pltpu.VMEM((T, QF), BF),
            pltpu.VMEM((T, S * W), BF),
            pltpu.VMEM((S, T, F), BF),
            pltpu.VMEM((D, 2, RP, LH + UH), BF),
            pltpu.VMEM((S, T, F), F32),
            pltpu.VMEM((T, D * RP), F32),
            pltpu.VMEM((T, LANES), F32),
            pltpu.VMEM((T, LANES), F32),
            pltpu.VMEM((T, hw), F32),
            pltpu.VMEM((T, hw), F32),
            pltpu.VMEM((ranks, T), BF),
            pltpu.VMEM((ranks, T), BF),
            pltpu.VMEM((S, small_rows, LANES), F32),
            pltpu.VMEM((S, small_rows, LANES), F32),
            pltpu.VMEM((small_rows, LANES), F32),
            pltpu.VMEM((D, small_rows, LANES), F32),
            pltpu.VMEM((small_rows, LANES), F32),
            pltpu.VMEM((S, small_rows, LANES), F32),
        ]
        + stage(F)
        + stage(W)
        + [dma((4,)), dma((S,)), dma((S,)), dma((D,)), dma((D,)), dma((D,)), dma((D,))]
        + [dma((S,)), dma((S,)), dma((D,)), dma((D,)), dma((S,)), dma((S,))]
        + [dma((2, K)), dma((2, K)), dma((2, K)), dma((2, K))]
        + [dma((2, D)), dma((2, D)), dma((2, S)), dma((2, S))],
        compiler_params=pltpu.CompilerParams(
            collective_id=0, has_side_effects=True, vmem_limit_bytes=56 * 1024 * 1024
        ),
    )(
        projections.reshape(T, QF),
        rotated_query_gradient.reshape(S, T, F),
        activations.reshape(T, M),
        adapt,
        gains,
        jnp.asarray(lane_frequencies()),
        positions.reshape(3, T),
        valid.reshape(1, T),
    )
    return down[None, :, :M], up[None], gain


def solution(mesh):
    in_specs = (
        P(None, "dp", "seq", None),
        P(None, "dp", None, "seq"),
        P(),
        P(None, "dp", None),
        P(None, "dp", None),
        P("dp", "seq", None),
        P(None, "dp", "seq"),
        P("dp", "seq"),
    )
    out_specs = (P(None, "dp", None), P(None, "dp", None), P())
    return jax.shard_map(shards, mesh=mesh, in_specs=in_specs, out_specs=out_specs, check_vma=False)
```

time: 217 us -> 51 us (0.24)
  blocking collectives: 99.5 us -> 0 us
  waiting for transfers between devices: 45.5 us -> 0 us
  Pallas kernels: 0 us -> 41 us
  other arithmetic: 22.5 us -> 0.79 us
  between operations: 15.3 us -> 0.65 us
  local copies, waits for them, and re-layouts: 22.7 us -> 8.15 us
  matrix products: 5.35 us -> 0 us
  starting transfers between devices: 5.32 us -> 0 us
    all_gather x4 -> x0, blocking collectives: 60.3 us -> none  [the longest x1 22.6 us: shards(): lax.all_gather(adapter_lowering, 'dp', axis=1, tiled=True)]
    pallas_call x0 -> x1, Pallas kernels: none -> 41 us  [shards(): pl.pallas_call(functools.partial(kernel, cfg), out_shape=(jax.ShapeDtypeS...]
    psum x1 -> x0, blocking collectives: 39.1 us -> none  [shards(): total_count = lax.psum(local_count, ('dp', 'seq'))]
    unnamed x4 -> x0, waiting for transfers between devices: 35.9 us -> none
    reduce_scatter x2 -> x0, waiting for transfers between devices: 9.65 us -> none  [the longest x1 9.63 us: shards(): lax.psum_scatter(lowering_portion, 'seq', scatter_dimension=2, tiled=True)]
    unnamed x22 -> x4, local copies, waits for them, and re-layouts: 14.6 us -> 6.33 us
    unnamed x1 -> x0, other arithmetic: 8.08 us -> none
    dot_general x2 -> x0, matrix products: 5.35 us -> none  [the longest x1 3.52 us: adapter_partial_terms(): jnp.dot(reduced.T, projection_change[0], preferred_element_type=jnp.float32)]
  transfers between devices with their start and end apart: 4 -> 0, of which waited for: 2 -> 0; matrix products, arithmetic and copies ran while one was open for 4% -> 0% of each run, Pallas kernels for 0% -> 0%
where the time goes in v1:
time: 51 us; the launch traced here: 50.6 us
  Pallas kernels  41 us (80%)
  local copies, waits for them, and re-layouts  8.15 us (16%)
  other arithmetic  0.79 us (2%)
  between operations  0.65 us (1%)
    pallas_call x1, Pallas kernels, shards(): pl.pallas_call(functools.partial(kernel, cfg), out_shape=(jax.ShapeDtypeS...  41 us
    unnamed x4, local copies, waits for them, and re-layouts  6.33 us

profile of v1, /device:TPU:0, one launch (start us, length us, event | category | flops | bytes accessed | tf_op | source)
XLA Modules:
  0.0 50.6 jit_solution(17297470221976704203)
XLA Ops:
  0.6 1.3 %copy.16 = s32[3,1,128]{2,0,1:T(4,128)} copy(s32[3,1,128]{2,1,0:T(1,128)} %param.15) | data formatting | bytes 3072
  1.9 0.9 %fusion.4 = (bf16[12,2048]{1,0:T(8,128)(2,1)S(1)}, bf16[12,2048]{1,0:T(8,128)(2,1)S(1)}) fusion(bf16[12,4096]{1,0:T(8,128)(2,1)} %bitcast.20), kind=kLoop, calls=%fused_computation.8 | loop fusion | bytes 196608 | tf_op jit(solution)/shard_map/slice | solution.py:383
  2.8 0.9 %fusion.3 = (bf16[12,2560]{1,0:T(8,128)(2,1)S(1)}, bf16[12,2560]{1,0:T(8,128)(2,1)S(1)}) fusion(bf16[12,5120]{1,0:T(8,128)(2,1)} %bitcast.19), kind=kLoop, calls=%fused_computation.7 | loop fusion | bytes 245760 | tf_op jit(solution)/shard_map/slice | solution.py:383
  3.8 0.8 %fusion.2.adapt_hbm = bf16[2,16,4608]{2,1,0:T(8,128)(2,1)} fusion(bf16[1,12,4608]{2,1,0:T(8,128)(2,1)S(1)} %get-tuple-element.17, bf16[1,12,4608]{2,1,0:T(8,128)(2,1)S(1)} %get-tuple-element.16), kind=kLoop, calls=%fused_computation.3 | loop fusion | flops 1032192 | bytes 516096 | tf_op jit(solution)/shard_map/stack | solution.py:382
  4.5 41.0 %shard_map.112 = (f32[12,5120]{1,0:T(8,128)}, f32[12,4096]{1,0:T(8,128)}, f32[1,4096]{1,0:T(1,128)}) custom-call(bf16[128,4096]{1,0:T(8,128)(2,1)} %bitcast.15, bf16[8,128,512]{2,1,0:T(8,128)(2,1)} %bitcast.16, bf16[128,5120]{1,0:T(8,128)(2,1)} %bitcast.14, bf16[2,16,4608]{2,1,0:T(8,128)(2,1)} %fusion.2.adapt_hbm, f32[1,4096]{1,0:T(1,128)} %gains_ref.1, ...), custom_call_target="tpu_custom_call" | custom-call | tf_op jit(solution)/shard_map/pallas_call | solution.py:407
  45.5 1.9 %copy.12 = f32[1,12,5120]{2,0,1:T(1,128)} copy(f32[1,12,5120]{2,1,0:T(8,128)} %bitcast.17) | data formatting | bytes 491520
  47.4 1.8 %copy.13 = f32[1,12,4096]{2,0,1:T(1,128)} copy(f32[1,12,4096]{2,1,0:T(8,128)} %bitcast.18) | data formatting | bytes 393216
  49.3 1.3 %copy.18 = f32[1,4096]{1,0:T(1,128)} copy(f32[1,4096]{1,0:T(1,128)} %get-tuple-element.23) | data formatting | bytes 32768
  (1 shorter events, 0.0 us)

commit v2 on v1

--- a/solution.py
+++ b/solution.py
@@ -31,9 +31,9 @@
 
 def kernel(
     cfg,
-    proj_hbm, cot_hbm, act_hbm, adapt_hbm, gains_ref, freq_ref, pos_ref, valid_ref,
+    proj_hbm, cot_hbm, act_hbm, low_hbm, rai_hbm, gains_ref, freq_ref, pos_ref, valid_ref,
     down_ref, up_ref, gain_ref,
-    proj, act, cot, adapt, scaled, back_acc, dot_acc, inv_ref, cos_ref, sin_ref, redt, backt,
+    proj, act, cot, cot_src, low, rai, fold, packed, adapt, scaled, back_acc, dot_acc, inv_ref, cos_ref, sin_ref, redt, backt,
     small_send, small_recv, small_dp, small_dp_recv, small_fin, small_ag,
     d2d_send_u, d2d_recv_u, own_u, rs_send_u, rs_recv_u, tot_u, dp_send_u, dp_f_u, dp_recv_u, ag_u, fin_u,
     d2d_send_d, d2d_recv_d, own_d, rs_send_d, rs_recv_d, tot_d, dp_send_d, dp_f_d, dp_recv_d, ag_d, fin_d,
@@ -41,8 +41,8 @@
     sm_s, sm_r, smd_s, smd_r, sma_s, sma_r,
     d2d_s, d2d_r, rs_s, rs_r, dp_s, dp_r, ag_s, ag_r,
 ):
-    S, D, T, F, W, R, RP, LH, M, QF = (
-        cfg[k] for k in ("S", "D", "T", "F", "W", "R", "RP", "LH", "M", "QF")
+    S, D, T, F, W, R, RP, LH, UH, M, QF, fd = (
+        cfg[k] for k in ("S", "D", "T", "F", "W", "R", "RP", "LH", "UH", "M", "QF", "fd")
     )
     K = S // 2
     ranks = D * R
@@ -62,27 +62,40 @@
     loads = [
         pltpu.make_async_copy(proj_hbm, proj, local_sem.at[0]),
         pltpu.make_async_copy(act_hbm, act.at[:, pl.ds(0, M)], local_sem.at[1]),
-        pltpu.make_async_copy(cot_hbm.at[s], cot.at[s], local_sem.at[2]),
-        pltpu.make_async_copy(adapt_hbm, adapt.at[d], local_sem.at[3]),
+        pltpu.make_async_copy(cot_hbm, cot_src, local_sem.at[2]),
+        pltpu.make_async_copy(low_hbm, low, local_sem.at[3]),
+        pltpu.make_async_copy(rai_hbm, rai, local_sem.at[4]),
     ]
-    for x in loads:
-        x.start()
+    for i in (3, 4, 2, 0, 1):
+        loads[i].start()
 
     barrier = pltpu.get_barrier_semaphore()
     for k in range(1, S):
         pl.semaphore_signal(barrier, inc=1, device_id=(d, lax.rem(s + k, S)), device_id_type=MESH)
     for k in range(1, D):
         pl.semaphore_signal(barrier, inc=1, device_id=(lax.rem(d + k, D), s), device_id_type=MESH)
+
+    LF, UF = LH // fd, UH // fd
+    fold[...] = jnp.zeros_like(fold)
+    loads[3].wait()
+    loads[4].wait()
+    for h in range(2):
+        for q in range(fd):
+            fold[q * R:(q + 1) * R, 0:LF] = low[:, h * LH + q * LF:h * LH + (q + 1) * LF].astype(F32)
+            fold[q * R:(q + 1) * R, LF:LF + UF] = rai[:, h * UH + q * UF:h * UH + (q + 1) * UF].astype(F32)
+        packed[d, h] = fold[0:packed.shape[2], :].astype(BF)
+
+    loads[2].wait()
     pl.semaphore_wait(barrier, S + D - 2)
 
     def cot_copy(peer, slot):
-        return copy(cot_hbm.at[peer], cot.at[slot], cot_s.at[peer], cot_r.at[slot], d, peer)
+        return copy(cot_src.at[peer], cot.at[slot], cot_s.at[peer], cot_r.at[slot], d, peer)
 
     def adapt_copy(peer, slot):
-        return copy(adapt_hbm.at[c], adapt.at[slot, c], ad_s.at[peer], ad_r.at[slot], peer, s)
+        return copy(packed.at[d, c], packed.at[slot, c], ad_s.at[peer], ad_r.at[slot], peer, s)
 
     def relay_copy(slot, half):
-        return copy(adapt.at[slot, half], adapt.at[slot, half], rel_s.at[slot], rel_r.at[slot], d, sib)
+        return copy(packed.at[slot, half], packed.at[slot, half], rel_s.at[slot], rel_r.at[slot], d, sib)
 
     for k in range(1, D):
         adapt_copy(lax.rem(d + k, D), d).start()
@@ -96,8 +109,8 @@
         return jnp.broadcast_to(row.astype(F32), (LANES, T)).T
 
     index = jnp.where(
-        lane < 2 * n0, column(pos_ref[0:1, :]),
-        jnp.where(lane < 2 * (n0 + n1), column(pos_ref[1:2, :]), column(pos_ref[2:3, :])),
+        lane < 2 * n0, column(pos_ref[0]),
+        jnp.where(lane < 2 * (n0 + n1), column(pos_ref[1]), column(pos_ref[2])),
     )
     angle = index * freq_ref[...]
     ok = column(valid_ref[...])
@@ -127,12 +140,12 @@
     def wide(x):
         return jnp.concatenate([x] * (hw // LANES), axis=1) if hw > LANES else x
 
-    def chunk(p):
+    def chunk(p, source=cot):
         inv = wide(inv_ref[...])
         cw, sw = cos_ref[...], sin_ref[...]
         for i in range(F // hw):
             cols = pl.ds(pl.multiple_of(p * F + i * hw, LANES), hw)
-            x = cot[p, :, i * hw:(i + 1) * hw]
+            x = source[p, :, i * hw:(i + 1) * hw]
             xs = jnp.dot(x, swap, preferred_element_type=F32)
             un = cw * x.astype(F32) + sw * xs
             prod = un * (proj[:, cols].astype(F32) * inv)
@@ -148,11 +161,9 @@
                 acc += pg[:, t * LANES:(t + 1) * LANES]
             dot_acc[...] += acc
 
-    loads[2].wait()
-    chunk(s)
+    chunk(s, cot_src)
     cot_copy(sib, sib).wait_recv()
     chunk(sib)
-    loads[3].wait()
 
     def rest(j, carry):
         p = lax.rem(2 * chip + 2 + j, S)
@@ -184,11 +195,22 @@
     for k in range(1, D):
         e = lax.rem(d + k, D)
         relay_copy(e, 1 - c).wait_recv()
+
+    def unfold(e, carry):
+        for h in range(2):
+            fold[0:packed.shape[2], :] = packed[e, h].astype(F32)
+            for q in range(fd):
+                rows = fold[q * R:q * R + RP, :].astype(BF)
+                adapt[e, h, :, q * LF:(q + 1) * LF] = rows[:, 0:LF]
+                adapt[e, h, :, LH + q * UF:LH + (q + 1) * UF] = rows[:, LF:LF + UF]
+        return carry
+
+    lax.fori_loop(0, D, unfold, 0)
     loads[1].wait()
     red = jnp.zeros((T, D * RP), F32)
     for h in range(2):
-        low = adapt[:, h, :, 0:LH].reshape(D * RP, LH)
-        red += lax.dot_general(act[:, h * LH:(h + 1) * LH], low, NT, preferred_element_type=F32)
+        lowering = adapt[:, h, :, 0:LH].reshape(D * RP, LH)
+        red += lax.dot_general(act[:, h * LH:(h + 1) * LH], lowering, NT, preferred_element_type=F32)
     redt[...] = dense_transposed(red)
 
     back_acc[...] = jnp.zeros_like(back_acc)
@@ -207,8 +229,8 @@
         delta = jnp.concatenate(parts, axis=1) if len(parts) > 1 else parts[0]
         h = p // K
         off = pl.multiple_of(LH + lax.rem(p, K) * F, LANES)
-        rai = adapt[:, h, :, pl.ds(off, F)].reshape(D * RP, F)
-        back_acc[...] += lax.dot_general(delta, rai, NT, preferred_element_type=F32)
+        raising = adapt[:, h, :, pl.ds(off, F)].reshape(D * RP, F)
+        back_acc[...] += lax.dot_general(delta, raising, NT, preferred_element_type=F32)
         return jnp.dot(redt[...], delta, preferred_element_type=F32)
 
     def down_term(p):
@@ -365,6 +387,13 @@
             rs_copy(b, k, chip).wait_send()
 
 
+def place(down_ref, up_ref, gain_ref, down_out, up_out, gain_out):
+    for r in range(down_out.shape[0]):
+        down_out[r] = down_ref[r:r + 1, 0:down_out.shape[2]]
+        up_out[r] = up_ref[r:r + 1, :]
+    gain_out[...] = gain_ref[...]
+
+
 def shards(projections, rotated_query_gradient, gains, adapter_lowering, adapter_raising,
            activations, positions, valid):
     D, S = lax.axis_size("dp"), lax.axis_size("seq")
@@ -376,13 +405,9 @@
     LH, UH = M // 2, QF // 2
     K = S // 2
     ranks = D * R
-    cfg = dict(S=S, D=D, T=T, F=F, W=W, R=R, RP=RP, LH=LH, M=M, QF=QF, tokens=D * S * T)
-
-    low, rai = adapter_lowering[0], adapter_raising[0]
-    adapt = jnp.stack(
-        [jnp.concatenate([low[:, h * LH:(h + 1) * LH], rai[:, h * UH:(h + 1) * UH]], 1) for h in range(2)]
-    )
-    adapt = jnp.pad(adapt, ((0, 0), (0, RP - R), (0, 0)))
+    fd = 4 if R % 4 == 0 and LH % (4 * LANES) == 0 and UH % (4 * LANES) == 0 else 1
+    folded = -(-fd * R // 16) * 16
+    cfg = dict(S=S, D=D, T=T, F=F, W=W, R=R, RP=RP, LH=LH, UH=UH, M=M, QF=QF, fd=fd, tokens=D * S * T)
 
     def stage(width):
         return [
@@ -411,12 +436,17 @@
             jax.ShapeDtypeStruct((R, QF), F32),
             jax.ShapeDtypeStruct((1, QF), F32),
         ),
-        in_specs=[any_space] * 4 + [vmem] * 4,
+        in_specs=[any_space] * 5 + [vmem] * 4,
         out_specs=(vmem, vmem, vmem),
         scratch_shapes=[
             pltpu.VMEM((T, QF), BF),
             pltpu.VMEM((T, S * W), BF),
             pltpu.VMEM((S, T, F), BF),
+            pltpu.VMEM((S, T, F), BF),
+            pltpu.VMEM((R, M), BF),
+            pltpu.VMEM((R, QF), BF),
+            pltpu.VMEM((folded + 16, (LH + UH) // fd), F32),
+            pltpu.VMEM((D, 2, folded, (LH + UH) // fd), BF),
             pltpu.VMEM((D, 2, RP, LH + UH), BF),
             pltpu.VMEM((S, T, F), F32),
             pltpu.VMEM((T, D * RP), F32),
@@ -435,7 +465,7 @@
         ]
         + stage(F)
         + stage(W)
-        + [dma((4,)), dma((S,)), dma((S,)), dma((D,)), dma((D,)), dma((D,)), dma((D,))]
+        + [dma((5,)), dma((S,)), dma((S,)), dma((D,)), dma((D,)), dma((D,)), dma((D,))]
         + [dma((S,)), dma((S,)), dma((D,)), dma((D,)), dma((S,)), dma((S,))]
         + [dma((2, K)), dma((2, K)), dma((2, K)), dma((2, K))]
         + [dma((2, D)), dma((2, D)), dma((2, S)), dma((2, S))],
@@ -446,13 +476,24 @@
         projections.reshape(T, QF),
         rotated_query_gradient.reshape(S, T, F),
         activations.reshape(T, M),
-        adapt,
+        adapter_lowering[0],
+        adapter_raising[0],
         gains,
         jnp.asarray(lane_frequencies()),
-        positions.reshape(3, T),
+        positions,
         valid.reshape(1, T),
     )
-    return down[None, :, :M], up[None], gain
+    down, up, gain = pl.pallas_call(
+        place,
+        out_shape=(
+            jax.ShapeDtypeStruct((R, 1, M), F32),
+            jax.ShapeDtypeStruct((R, 1, QF), F32),
+            jax.ShapeDtypeStruct((1, QF), F32),
+        ),
+        in_specs=[vmem] * 3,
+        out_specs=(vmem, vmem, vmem),
+    )(down, up, gain)
+    return down.reshape(1, R, M), up.reshape(1, R, QF), gain
 
 
 def solution(mesh):

time: 51 us -> 42.9 us (0.84)
  local copies, waits for them, and re-layouts: 8.15 us -> 0 us
  Pallas kernels: 41 us -> 42.1 us
  other arithmetic: 0.79 us -> 0 us
    unnamed x4 -> x0, local copies, waits for them, and re-layouts: 6.33 us -> none
    pallas_call x0 -> x1, Pallas kernels: none -> 1.85 us  [shards(): pl.pallas_call(place, out_shape=(jax.ShapeDtypeStruct((R, 1, M), F32), ja...]
    slice x2 -> x0, local copies, waits for them, and re-layouts: 1.82 us -> none  [the longest x1 0.94 us: shards(): low[:, h * LH:(h + 1) * LH]]
    another operation x2 -> x0, other arithmetic: 0.79 us -> none  [shards(): jnp.stack([jnp.concatenate([low[:, h * LH:(h + 1) * LH], rai[:, h * UH:(h...]
    pallas_call x1, Pallas kernels: 41 us -> 40.2 us  [shards(): pl.pallas_call(functools.partial(kernel, cfg), out_shape=(jax.ShapeDtypeS...]
where the time goes in v2:
time: 42.9 us; the launch traced here: 42.7 us
  Pallas kernels  42.1 us (98%)
  between operations  0.64 us (1%)
    pallas_call x1, Pallas kernels, shards(): pl.pallas_call(functools.partial(kernel, cfg), out_shape=(jax.ShapeDtypeS...  40.2 us
    pallas_call x1, Pallas kernels, shards(): pl.pallas_call(place, out_shape=(jax.ShapeDtypeStruct((R, 1, M), F32), ja...  1.85 us

profile of v2, /device:TPU:0, one launch (start us, length us, event | category | flops | bytes accessed | tf_op | source)
XLA Modules:
  0.0 42.7 jit_solution(10315229973457463490)
XLA Ops:
  0.6 40.2 %shard_map.112 = (f32[12,5120]{1,0:T(8,128)}, f32[12,4096]{1,0:T(8,128)}, f32[1,4096]{1,0:T(1,128)}) custom-call(bf16[128,4096]{1,0:T(8,128)(2,1)} %bitcast.8, bf16[8,128,512]{2,1,0:T(8,128)(2,1)} %bitcast.9, bf16[128,5120]{1,0:T(8,128)(2,1)} %bitcast.7, bf16[12,5120]{1,0:T(8,128)(2,1)} %bitcast.10, bf16[12,4096]{1,0:T(8,128)(2,1)} %bitcast.11, ...), custom_call_target="tpu_custom_call" | custom-call | tf_op jit(solution)/shard_map/pallas_call | solution.py:432
  40.9 1.9 %shard_map.113 = (f32[12,1,5120]{2,1,0:T(1,128)}, f32[12,1,4096]{2,1,0:T(1,128)}, f32[1,4096]{1,0:T(1,128)}) custom-call(f32[12,5120]{1,0:T(8,128)} %get-tuple-element.9.down_ref, f32[12,4096]{1,0:T(8,128)} %get-tuple-element.10.up_ref, f32[1,4096]{1,0:T(1,128)} %get-tuple-element.11.gain_ref), custom_call_target="tpu_custom_call" | custom-call | tf_op jit(solution)/shard_map/pallas_call | solution.py:486
